TPU v7x, 8 devices: a whole 2x2x1 slice. The times are simulated.
8 devices in a mesh: col: 4 (over z, y, x), row: 2 (over core).
Axes of the slice: x: 2, y: 2, z: 1, core: 2. Of those that a mesh axis runs over, the one named last changes fastest.
Arguments:
- t_amp: float32 [1024, 20736], P('row', 'col')
- d_denom: float32 [1024, 20736], P('row', 'col')
- v_oovv: bfloat16 [1024, 20736], P('row', 'col')
- v_vvvv: bfloat16 [20736, 20736], P('row', 'col')
- v_oooo: bfloat16 [1024, 1024], replicated
- w_ovov: bfloat16 [4608, 4608], P(None, 'col')
Outputs:
- output: float32 [4608, 4608], P('row', 'col')
All inputs are finite; a program needn't handle non-finite values.
Results may differ from a plain program's by a relative error of at most 0.001.
Values are sent between devices in bfloat16 or wider.
A program may use at most 1 GiB of HBM per device.

v0:
```python
import math
import jax
import jax.numpy as jnp
from jax import lax
from jax.sharding import PartitionSpec as P


def solution(mesh):
    row_n = mesh.shape["row"]
    col_n = mesh.shape["col"]

    def local_sweep(t_blk, d_blk, voovv_blk, vvvvv_blk, oooo_blk, wr_blk):
        n_occ = math.isqrt(oooo_blk.shape[0])
        n_vir = wr_blk.shape[0] // n_occ
        occ_r = n_occ // row_n
        occ_c = n_occ // col_n
        vir_c = n_vir // col_n
        t_bf = t_blk.astype(jnp.bfloat16)
        t_rows = lax.all_gather(t_bf, "col", axis=1, tiled=True)
        t_ladder = lax.all_to_all(t_rows, "row", 1, 0, tiled=True)
        ladder_part = jnp.dot(t_ladder, vvvvv_blk, preferred_element_type=jnp.float32)
        r_ladder = lax.psum_scatter(ladder_part, "row", scatter_dimension=0, tiled=True)
        t_cols = lax.all_gather(t_bf, "row", axis=0, tiled=True)
        x_part = lax.dot_general(voovv_blk, t_cols, (((1,), (1,)), ((), ())), preferred_element_type=jnp.float32)
        x_rows = lax.psum(x_part, "col")
        x_cols = lax.all_to_all(x_rows, "row", 1, 0, tiled=True)
        w_hole = (oooo_blk.astype(jnp.float32) + 0.5 * x_cols).astype(jnp.bfloat16)
        r_hole = lax.dot_general(w_hole, t_cols, (((0,), (0,)), ((), ())), preferred_element_type=jnp.float32)
        amp_four = t_rows.reshape(occ_r, n_occ, n_vir, n_vir)
        wr_three = wr_blk.reshape(n_occ, n_vir, occ_c * n_vir)
        r_mixed = jnp.einsum("ikac,kcn->ian", amp_four, wr_three, preferred_element_type=jnp.float32)
        r_mixed = r_mixed.reshape(occ_r, n_vir, occ_c, n_vir)
        mixed_entry = lax.all_to_all(r_mixed, "col", 1, 2, tiled=True)
        swap_rows = lax.all_to_all(mixed_entry, "row", 2, 0, tiled=True)
        swap_full = lax.all_to_all(swap_rows, "col", 3, 1, tiled=True)
        mixed_image = jnp.transpose(swap_full, (2, 3, 0, 1))
        base_sum = (voovv_blk.astype(jnp.float32) + r_ladder + r_hole).reshape(occ_r, n_occ, vir_c, n_vir)
        d_four = d_blk.reshape(occ_r, n_occ, vir_c, n_vir)
        total_sum = (jnp.transpose(base_sum, (0, 2, 1, 3)) + mixed_entry + mixed_image) / jnp.transpose(d_four, (0, 2, 1, 3))
        t_pairs = lax.all_to_all(total_sum, "col", 2, 1, tiled=True)
        return t_pairs.reshape(occ_r * n_vir, occ_c * n_vir)

    return jax.shard_map(
        local_sweep,
        mesh=mesh,
        in_specs=(P("row", "col"), P("row", "col"), P("row", "col"), P("row", "col"), P(None, "row"), P(None, "col")),
        out_specs=P("row", "col"),
        check_vma=False,
    )
```

profile of v0, /device:TPU:0, one launch (start us, length us, event | category | flops | bytes accessed | tf_op | source)
XLA Modules:
  0.0 1823.2 jit_solution(4805639225445062191)
XLA Ops:
  14.4 23.1 %all-gather.5.cloned.1.call-done = bf16[1024,5184]{0,1:T(8,128)(2,1)} async-done(((bf16[512,5184]{0,1:T(8,128)(2,1)}), bf16[1024,5184]{0,1:T(8,128)(2,1)}) %all-gather.5.cloned.1.call-update) | async-done | bytes 10616848 | tf_op jit(solution)/shard_map/all_gather | solution.py:23
  49.4 181.0 %all-gather.3.cloned.1.call-done = bf16[512,20736]{0,1:T(8,128)(2,1)} async-done(((bf16[512,5184]{0,1:T(8,128)(2,1)}), bf16[512,20736]{0,1:T(8,128)(2,1)}) %all-gather.3.cloned.1.call-update) | async-done | bytes 21233680 | tf_op jit(solution)/shard_map/all_gather | solution.py:19
  230.3 38.9 %all_to_all.101 = bf16[512,2,10368]{0,2,1:T(8,128)(2,1)} all-to-all(bf16[512,2,10368]{0,2,1:T(8,128)(2,1)} %bitcast.78), channel_id=1, replica_groups=mesh['col'=4,'row'=2] {'row'}, dimensions={1} | all-to-all | bytes 42467328 | tf_op jit(solution)/shard_map/all_to_all | solution.py:20
  269.2 25.6 %copy.59 = bf16[2,512,10368]{2,1,0:T(8,128)(2,1)} copy(bf16[2,512,10368]{1,2,0:T(8,128)(2,1)} %bitcast.79) | data formatting | bytes 42467328 | tf_op jit(solution)/shard_map/all_to_all | solution.py:20
  294.8 125.7 %fusion.9 = f32[1024,5184]{0,1:T(8,128)} fusion(bf16[1024,10368]{1,0:T(8,128)(2,1)} %bitcast.84, bf16[10368,5184]{0,1:T(8,128)(2,1)} %param.9), kind=kOutput, calls=%fused_computation.15 | convolution fusion | flops 110075314176 | bytes 149962752 | tf_op jit(solution)/shard_map/dot_general | solution.py:21
  420.5 13.2 copy.96
  433.7 32.8 %dot_general.20 = bf16[8,144,144,32]{1,0,3,2:T(8,128)(2,1)} reshape(bf16[1152,144,32]{0,2,1:T(8,128)(2,1)} %bitcast.83) | data formatting | bytes 21233664 | tf_op jit(solution)/shard_map/ikac,kcn->ian/dot_general | solution.py:31
  466.5 29.7 %copy.64 = bf16[8,144,144,32]{2,1,3,0:T(8,128)(2,1)} copy(bf16[8,144,144,32]{1,0,3,2:T(8,128)(2,1)} %dot_general.20) | data formatting | bytes 21233664 | tf_op jit(solution)/shard_map/ikac,kcn->ian/dot_general | solution.py:31
  496.2 25.8 %copy.62 = bf16[512,20736]{1,0:T(8,128)(2,1)} copy(bf16[512,20736]{0,1:T(8,128)(2,1)} %all-gather.3.cloned.1.call-done) | data formatting | bytes 42467328 | tf_op jit(solution)/shard_map/all_gather | solution.py:19
  521.9 67.4 %reshape.41 = bf16[16,32,144,144,1]{3,2,1,0,4:T(8,128)(2,1)} reshape(bf16[512,20736]{1,0:T(8,128)(2,1)} %copy.62) | data formatting | bytes 42467328 | tf_op jit(solution)/shard_map/reshape | solution.py:29
  589.4 87.1 %fusion.3 = f32[16,144,8,144]{3,1,2,0:T(8,128)} fusion(bf16[8,144,144,32]{2,1,3,0:T(8,128)(2,1)} %copy.64, bf16[16,32,144,144,1]{3,2,1,0,4:T(8,128)(2,1)} %reshape.41), kind=kOutput, calls=%fused_computation.10 | convolution fusion | flops 24461180928 | bytes 42467328 | tf_op jit(solution)/shard_map/ikac,kcn->ian/dot_general | solution.py:31
  676.5 14.1 copy.65
  690.6 209.1 %all_to_all.102 = f32[16,144,8,144]{3,2,0,1:T(8,128)S(1)} all-to-all(f32[16,144,8,144]{3,2,0,1:T(8,128)S(1)} %copy.65), channel_id=1, replica_groups=mesh['col'=4,'row'=2] {'col'}, dimensions={1} | all-to-all | bytes 21233664 | tf_op jit(solution)/shard_map/all_to_all | solution.py:33
  908.4 21.5 %copy.69 = f32[16,36,32,144]{3,0,1,2:T(8,128)} copy(f32[16,36,32,144]{3,2,1,0:T(8,128)S(1)} %bitcast.73) | data formatting | bytes 21233664 | tf_op jit(solution)/shard_map/all_to_all | solution.py:33
  940.3 14.6 all-to-all-done.3
  958.7 19.5 %copy.71 = f32[2,16,36,16,144]{4,3,2,1,0:T(8,128)} copy(f32[2,16,36,16,144]{4,1,2,3,0:T(8,128)} %bitcast.19) | data formatting | bytes 21233664 | tf_op jit(solution)/shard_map/all_to_all | solution.py:34
  978.2 28.8 %copy.72 = f32[32,36,16,144]{1,2,0,3:T(8,128)} copy(f32[32,36,16,144]{3,2,1,0:T(8,128)} %bitcast.80) | data formatting | bytes 21233664 | tf_op jit(solution)/shard_map/all_to_all | solution.py:34
  1007.0 70.6 %reshape.45 = f32[4,1,663552]{2,1,0:T(1,128)} reshape(f32[144,32,16,36]{3,2,1,0:T(8,128)} %bitcast.75) | data formatting | bytes 21233664
  1085.1 11.6 copy.76
  1096.7 19.3 %reshape.31 = f32[16,32,36,144]{3,2,1,0:T(8,128)} reshape(f32[512,5184]{1,0:T(8,128)} %copy.76) | data formatting | bytes 21233664 | tf_op jit(solution)/shard_map/reshape | solution.py:38
  1118.0 82.8 %all-to-all-done.4 = f32[4,1,663552]{2,1,0:T(1,128)} async-done(((f32[4,1,663552]{2,1,0:T(1,128)}), f32[4,1,663552]{2,1,0:T(1,128)}, u32[]{:S(2)}, u32[]{:S(2)}) %all-to-all-start.4) | async-done | bytes 10616864 | tf_op jit(solution)/shard_map/all_to_all | solution.py:35
  1201.4 115.0 %reduce = f32[4,663552]{1,0:T(4,128)} reduce(f32[4,1,663552]{2,1,0:T(1,128)} %all-to-all-done.4, f32[]{:T(128)} %broadcast.5), dimensions={1}, to_apply=%all_to_all.88.reduce_sub_computation | reduce | bytes 21233668 | tf_op jit(solution)/shard_map/all_to_all | solution.py:35
  1316.4 72.2 %reshape.46 = f32[144,32,16,36]{3,2,1,0:T(8,128)} reshape(f32[4,663552]{1,0:T(4,128)} %reduce) | data formatting | bytes 21233664
  1388.6 42.9 %copy.94 = f32[32,36,16,4,36]{1,3,2,4,0:T(4,128)} copy(f32[32,36,16,4,36]{1,2,0,4,3:T(8,128)} %bitcast.76) | data formatting | bytes 21233664 | tf_op jit(solution)/shard_map/all_to_all | solution.py:35
  1431.4 32.6 %all_to_all.91 = f32[32,144,16,36]{1,2,3,0:T(8,128)} reshape(f32[32,4,36,16,36]{2,1,3,4,0:T(4,128)} %bitcast.77) | data formatting | bytes 21233664 | tf_op jit(solution)/shard_map/all_to_all | solution.py:35
  1464.1 14.6 add_add_fusion
  1490.4 19.3 %reshape.28 = f32[16,32,36,144]{3,2,1,0:T(8,128)} reshape(f32[512,5184]{1,0:T(8,128)} %copy.61) | data formatting | bytes 21233664 | tf_op jit(solution)/shard_map/reshape | solution.py:37
  1509.6 42.1 %bitcast_divide_fusion = f32[16,36,32,144]{3,1,2,0:T(8,128)} fusion(f32[16,32,36,144]{3,2,1,0:T(8,128)} %reshape.31, f32[16,32,36,144]{3,2,1,0:T(8,128)} %reshape.28, f32[32,144,16,36]{1,2,3,0:T(8,128)} %all_to_all.91, f32[16,36,32,144]{3,2,1,0:T(8,128)} %bitcast.74), kind=kLoop, calls=%fused_computation.3 | loop fusion | flops 7962624 | bytes 53084160 | tf_op jit(solution)/shard_map/div | solution.py:39
  1551.8 17.1 copy.77
  1568.9 210.0 %all_to_all.103 = f32[16,36,32,144]{3,0,1,2:T(8,128)} all-to-all(f32[16,36,32,144]{3,0,1,2:T(8,128)S(1)} %copy.77), channel_id=1, replica_groups=mesh['col'=4,'row'=2] {'col'}, dimensions={2} | all-to-all | bytes 21233664 | tf_op jit(solution)/shard_map/all_to_all | solution.py:40
  1778.9 19.7 %copy.79 = f32[16,4,36,8,144]{4,3,2,1,0:T(8,128)} copy(f32[16,4,36,8,144]{4,0,2,3,1:T(8,128)} %bitcast.82) | data formatting | bytes 21233664 | tf_op jit(solution)/shard_map/all_to_all | solution.py:40
  1798.6 17.8 reshape.32
  (27 shorter events, 63.4 us)
Async XLA Ops:
  6.5 31.1 %all-gather.5.cloned.1.call-start = ((), (), s32[]{:S(2)}) async-start(), calls=%async_computation.9 | async-start | bytes 15925248 | tf_op jit(solution)/shard_map/all_gather | solution.py:23
  13.6 216.7 %all-gather.3.cloned.1.call-start = ((), (), s32[]{:S(2)}) async-start(), calls=%async_computation.7 | async-start | bytes 26542080 | tf_op jit(solution)/shard_map/all_gather | solution.py:19
  14.4 925.9 %all-reduce.2.cloned.1.call-start = ((), (), s32[]{:S(2)}) async-start(), calls=%async_computation.10 | async-start | bytes 4194304 | tf_op jit(solution)/shard_map/psum | solution.py:25
  49.3 1414.8 %reduce-scatter.2.cloned.1.call-start = ((), (), s32[]{:S(2)}) async-start(), calls=%async_computation.8 | async-start | bytes 31850496 | tf_op jit(solution)/shard_map/reduce_scatter | solution.py:22
  902.0 6.4 copy-start
  929.9 25.0 %all-to-all-start.3 = ((f32[16,36,32,144]{3,0,1,2:T(8,128)}), f32[16,36,32,144]{3,0,1,2:T(8,128)}, u32[]{:S(2)}, u32[]{:S(2)}) async-start(f32[16,36,32,144]{3,0,1,2:T(8,128)} %copy.69), calls=%async_computation.4 | async-start | bytes 37748736 | tf_op jit(solution)/shard_map/all_to_all | solution.py:34
  954.9 122.8 %all-to-all-start.1 = ((f32[512,2,512]{2,0,1:T(8,128)}), f32[512,2,512]{2,0,1:T(8,128)S(1)}, u32[]{:S(2)}, u32[]{:S(2)}) async-start(f32[512,2,512]{2,0,1:T(8,128)} %all-reduce.2.cloned.1.call-done), calls=%async_computation.2 | async-start | bytes 4194304 | tf_op jit(solution)/shard_map/all_to_all | solution.py:26
  1077.7 6.1 copy-start.1
  1077.7 123.1 %all-to-all-start.4 = ((f32[4,1,663552]{2,1,0:T(1,128)}), f32[4,1,663552]{2,1,0:T(1,128)}, u32[]{:S(2)}, u32[]{:S(2)}) async-start(f32[4,1,663552]{2,1,0:T(1,128)} %reshape.45), calls=%async_computation.5 | async-start | bytes 21233664 | tf_op jit(solution)/shard_map/all_to_all | solution.py:35
Sparse Core Ops, SparseCore 0:
  13.8 23.7 all-gather.4
  39.4 190.9 all-gather.2
  233.4 57.8 all-reduce.1
  420.7 24.6 reduce-scatter.1
where the time goes:
time: 1830 us; the launch traced here: 1820 us
  local copies, waits for them, and re-layouts  625 us (34%)
  blocking collectives  458 us (25%)
  waiting for transfers between devices  302 us (17%)
  matrix products  238 us (13%)
  other arithmetic  166 us (9%)
  starting transfers between devices  20.3 us (1%)
    all_to_all x1, blocking collectives, local_sweep(): t_pairs = lax.all_to_all(total_sum, 'col', 2, 1, tiled=True)  210 us
    all_to_all x1, blocking collectives, local_sweep(): mixed_entry = lax.all_to_all(r_mixed, 'col', 1, 2, tiled=True)  209 us
    all_gather x1, waiting for transfers between devices, local_sweep(): t_rows = lax.all_gather(t_bf, 'col', axis=1, tiled=True)  181 us
    unnamed x7, local copies, waits for them, and re-layouts  161 us
    dot_general x1, matrix products, local_sweep(): jnp.dot(t_ladder, vvvvv_blk, preferred_element_type=jnp.float32)  126 us
    all_to_all x1, other arithmetic, local_sweep(): swap_full = lax.all_to_all(swap_rows, 'col', 3, 1, tiled=True)  115 us
    dot_general x1, matrix products, local_sweep(): jnp.einsum('ikac,kcn->ian', amp_four, wr_three, preferred_element_type=jn...  87.1 us
    all_to_all x1, waiting for transfers between devices, local_sweep(): swap_full = lax.all_to_all(swap_rows, 'col', 3, 1, tiled=True)  82.8 us
  transfers between devices with their start and end apart: 7, of which 4 were waited for; matrix products, arithmetic and copies ran while one was open for 46% of the time, Pallas kernels for 0%

commit v1 on v0

v1 whole, which is shorter than its diff:
```python
import functools
import jax
import jax.numpy as jnp
from jax import lax
from jax.experimental import pallas as pl
from jax.experimental.pallas import tpu as pltpu
from jax.sharding import PartitionSpec as P


F32 = jnp.float32
BF = jnp.bfloat16


def cost(nbytes, us):
    return pl.CostEstimate(flops=int(us * 6e7), bytes_accessed=nbytes, transcendentals=0)


def put_rows(x, scr, scr2, n_i, pitch):
    m, t = x[:128].T, x[128:].T
    for i in range(n_i):
        scr[i * pitch : i * pitch + 32] = m[i * 32 : (i + 1) * 32]
        scr2[i * pitch : i * pitch + 32, :16] = t[i * 32 : (i + 1) * 32]


def d_kernel(x_ref, o_ref, scr, scr2, *, na, pitch):
    @pl.loop(0, na)
    def _(q):
        put_rows(x_ref[q], scr, scr2, 16, pitch)
        for j in range(32):
            c, jj = divmod(j, 8)
            for g in range(2):
                rows = pl.ds(j + g * 8 * pitch, 8, stride=pitch)
                o_ref[c, g, q, :, jj * 144 : jj * 144 + 128] = scr[rows, :]
                o_ref[c, g, q, :, jj * 144 + 128 : (jj + 1) * 144] = scr2[rows, :][:, :16]


def regroup_d(x, na=4, pitch=40):
    return pl.pallas_call(
        functools.partial(d_kernel, na=na, pitch=pitch),
        grid=(36 // na,),
        in_specs=[pl.BlockSpec((na, 144, 512), lambda i: (i, 0, 0))],
        out_specs=pl.BlockSpec((4, 2, na, 8, 1152), lambda i: (0, 0, i, 0, 0)),
        out_shape=jax.ShapeDtypeStruct((4, 2, 36, 8, 1152), F32),
        scratch_shapes=[pltpu.VMEM((16 * pitch, 128), F32)] * 2,
        cost_estimate=cost(2 * 10616832, 17),
    )(x)


def base_kernel(s_ref, p_ref, q_ref, v_ref, al, ah, bl, bh, o_ref, scr, scr2, *, na, pitch):
    own = s_ref[0]

    @pl.loop(0, na)
    def _(q):
        put_rows(p_ref[q] + q_ref[q] + v_ref[q], scr, scr2, 8, pitch)
        for j in range(32):
            c, jj = divmod(j, 8)
            rows = pl.ds(j, 8, stride=pitch)
            o_ref[c, q, :, jj * 144 : jj * 144 + 128] = scr[rows, :]
            o_ref[c, q, :, jj * 144 + 128 : (jj + 1) * 144] = scr2[rows, :][:, :16]
        for c in range(4):
            pair = ((al, bl), (ah, bh))[c % 2]

            @pl.when(own == c // 2)
            def _():
                o_ref[c, q] += pair[0][0, 0, q]

            @pl.when(own != c // 2)
            def _():
                o_ref[c, q] += pair[1][0, 0, q]


def regroup_base(g, s, p, q, v, imgs, na=4, pitch=40):
    own = pl.BlockSpec((1, 1, na, 8, 1152), lambda i, s: (s[0], g, i, 0, 0))
    im = pl.BlockSpec((1, 1, na, 8, 1152), lambda i, s: (0, g, i, 0, 0))
    return pl.pallas_call(
        functools.partial(base_kernel, na=na, pitch=pitch),
        grid_spec=pltpu.PrefetchScalarGridSpec(
            num_scalar_prefetch=1,
            grid=(36 // na,),
            in_specs=[
                pl.BlockSpec((na, 144, 256), lambda i, s: (i, 0, 0)),
                pl.BlockSpec((na, 144, 256), lambda i, s: (i, 0, 1)),
                pl.BlockSpec((na, 144, 256), lambda i, s: (i, 0, g)),
                own, own, im, im,
            ],
            out_specs=pl.BlockSpec((4, na, 8, 1152), lambda i, s: (0, i, 0, 0)),
            scratch_shapes=[pltpu.VMEM((8 * pitch, 128), F32)] * 2,
        ),
        out_shape=jax.ShapeDtypeStruct((4, 36, 8, 1152), F32),
        cost_estimate=cost(5 * 5308416, 16),
    )(s, p, q, v, *imgs)


def mix_kernel(x_ref, *rest, nb, nj, pitch):
    o_ref, scr, scr2 = rest[-3:]

    @pl.loop(0, nb)
    def _(q):
        rows = pl.ds(pl.multiple_of(q * pitch, 8), nj * 32)
        scr[rows, :] = x_ref[q, :128].T.astype(F32)
        scr2[rows, :16] = x_ref[q, 128:].T.astype(F32)

    @pl.loop(0, nj)
    def _(j):
        for k in range(32):
            rows = pl.ds(j * 32 + k, nb, stride=pitch)
            o_ref[j, :, k * 144 : k * 144 + 128] = scr[rows, :].astype(BF)
            o_ref[j, :, k * 144 + 128 : (k + 1) * 144] = scr2[rows, :][:, :16].astype(BF)


def mix(x, part=0, prev=None, nb=16):
    nj = x.shape[-1] // 32
    pitch = nj * 32 + 8
    in_specs = [pl.BlockSpec((nb, 144, nj * 32), lambda i: (i, 0, 0))]
    args, alias = [x], {}
    if prev is not None:
        in_specs += [pl.BlockSpec(memory_space=pl.ANY)]
        args, alias = [x, prev], {1: 0}
    return pl.pallas_call(
        functools.partial(mix_kernel, nb=nb, nj=nj, pitch=pitch),
        grid=(144 // nb,),
        in_specs=in_specs,
        out_specs=pl.BlockSpec((nj, nb, 4608), lambda i: (part, i, 0)),
        out_shape=jax.ShapeDtypeStruct((8, 144, 4608), BF),
        scratch_shapes=[pltpu.VMEM((nb * pitch, 128), F32)] * 2,
        input_output_aliases=alias,
        cost_estimate=cost(nj * 2654208, nj * 3.6),
    )(*args)


def wt_kernel(w_ref, o_ref, scr):
    for h in range(2):
        scr[...] = w_ref[h * 128 : (h + 1) * 128].astype(F32).T
        for a in range(0, 144, 2):
            v = jnp.concatenate([scr[pl.ds(a, 8, stride=144), :], scr[pl.ds(a + 1, 8, stride=144), :]], axis=0)
            o_ref[a * 8 : a * 8 + 16, h * 128 : (h + 1) * 128] = v.astype(BF)


def w_rows(w):
    return pl.pallas_call(
        wt_kernel,
        grid=(18,),
        in_specs=[pl.BlockSpec((256, 1152), lambda i: (i, 0))],
        out_specs=pl.BlockSpec((1152, 256), lambda i: (0, i)),
        out_shape=jax.ShapeDtypeStruct((1152, 4608), BF),
        scratch_shapes=[pltpu.VMEM((1152, 128), F32)],
        cost_estimate=cost(2 * 10616832, 19),
    )(w)


def place_kernel(s_ref, *refs):
    o_ref = refs[-1]
    for n in range(8):
        @pl.when(pl.program_id(0) == n)
        def _():
            o_ref[0] = refs[n].at[0][...]


def place(idx, own, got, oth):
    def one(f):
        return pl.BlockSpec((1, 144, 4608), f)

    specs = [one(lambda n, s: (2 * s[8], 0, 0)), one(lambda n, s: (2 * s[8] + 1, 0, 0))]
    specs += [one(lambda n, s: (0, 0, 0))] * 6
    return pl.pallas_call(
        place_kernel,
        grid_spec=pltpu.PrefetchScalarGridSpec(
            num_scalar_prefetch=1,
            grid=(8,),
            in_specs=specs,
            out_specs=pl.BlockSpec((1, 144, 4608), lambda n, s: (s[n], 0, 0)),
        ),
        out_shape=jax.ShapeDtypeStruct((8, 144, 4608), BF),
        cost_estimate=cost(2 * 10616832, 8),
    )(idx, own, own, *got, *oth)


def fin_kernel(c_ref, b0, b1, b2, b3, d0, d1, d2, d3, r_ref, *rest):
    o_ref, ns, ds = rest[-3:]
    c = c_ref[0]
    lanes = o_ref.shape[-1]
    for m, (b, d) in enumerate(((b0, d0.at[0, 0]), (b1, d1.at[0]), (b2, d2.at[0]), (b3, d3.at[0]))):
        rows = pl.ds(pl.multiple_of((c ^ m) * 288, 8), 288)
        ns[rows, :] = b[...].reshape(288, lanes)
        ds[rows, :] = d[...].reshape(288, lanes)

    @pl.loop(0, 8)
    def _(i):
        for a in range(0, 144, 8):
            rows = pl.ds(a * 8 + i, 8, stride=8)
            o_ref[i, a : a + 8, :] = (ns[rows, :] + r_ref[i, a : a + 8, :]) / ds[rows, :]


def finish(g, cidx, b_own, b_got, d_all, d_got, r3, prev=None, lanes=128):
    in_specs = [pl.BlockSpec((36, 8, lanes), lambda l, c: (0, 0, l))] * 4
    in_specs += [pl.BlockSpec((1, 1, 36, 8, lanes), lambda l, c: (c[0], g, 0, 0, l))]
    in_specs += [pl.BlockSpec((1, 36, 8, lanes), lambda l, c: (g, 0, 0, l))] * 3
    in_specs += [pl.BlockSpec((8, 144, lanes), lambda l, c: (0, 0, l))]
    args = [cidx, b_own, *b_got, d_all, *d_got, r3]
    alias = {}
    if prev is not None:
        in_specs += [pl.BlockSpec(memory_space=pl.ANY)]
        alias = {len(args): 0}
        args += [prev]
    return pl.pallas_call(
        fin_kernel,
        grid_spec=pltpu.PrefetchScalarGridSpec(
            num_scalar_prefetch=1,
            grid=(1152 // lanes,),
            in_specs=in_specs,
            out_specs=pl.BlockSpec((8, 144, lanes), lambda l, c: (g, 0, l)),
            scratch_shapes=[pltpu.VMEM((1152, lanes), F32)] * 2,
        ),
        out_shape=jax.ShapeDtypeStruct((16, 144, 1152), F32),
        input_output_aliases=alias,
        cost_estimate=cost(4 * 5308416, 10),
    )(*args)


def solution(mesh):
    col_n = mesh.shape["col"]
    flip = [(0, 1), (1, 0)]

    def hop(x, m):
        return lax.ppermute(x, "col", [(i, i ^ m) for i in range(col_n)])

    def swap(x):
        return lax.ppermute(x, "row", flip)

    def pick(x, i):
        return lax.dynamic_index_in_dim(x, i, 0, keepdims=False)

    def mm(a, b, dims):
        return lax.dot_general(a, b, (dims, ((), ())), preferred_element_type=F32)

    fence = lax.optimization_barrier

    def sweep(t_blk, d_blk, voovv_blk, vvvvv_blk, oooo, w_blk):
        c = lax.axis_index("col")
        r = lax.axis_index("row")
        t_own = t_blk.T.astype(BF)
        d_t, v_t, vv_t = d_blk.T, voovv_blk.T, vvvvv_blk.T
        gather = functools.partial(lax.all_gather, axis_name="col", axis=0, tiled=True)
        t_a = gather(t_own[:, :128])
        t_b = gather(t_own[:, 128:256])
        t_hi = gather(t_own[:, 256:])
        t_cat = jnp.concatenate([t_own, swap(t_own)], axis=1)
        x_part = mm(v_t, t_cat, ((0,), (0,))).reshape(4, 128, 1024)
        wt_all = w_rows(w_blk).reshape(8, 144, 4608)
        d_all = regroup_d(d_t.reshape(36, 144, 512))

        def half(t, who):
            return lax.dynamic_slice(t, (who * 10368, 0), (10368, t.shape[1]))

        x_out = [pick(x_part, c ^ m) for m in range(4)]
        w_out = [pick(wt_all, 2 * (c ^ m) + r) for m in (1, 2, 3)]
        d_out = [pick(d_all, c ^ m) for m in (1, 2, 3)]
        t_a, w_out, d_out, x_out = fence((t_a, w_out, d_out, x_out))
        s_a = swap(half(t_a, 1 - r))
        mix_lo = mix(t_a.reshape(144, 144, 128))
        t_b, x_out, mix_lo = fence((t_b, x_out, mix_lo))
        x_got = [hop(x_out[m], m) for m in (1, 2, 3)]
        s_b = swap(half(t_b, 1 - r))
        mix_lo = mix(t_b.reshape(144, 144, 128), 1, mix_lo).reshape(1152, 4608)
        x_sum = x_out[0] + x_got[0] + x_got[1] + x_got[2]
        o_rows = lax.dynamic_slice(oooo, (r * 512 + c * 128, 0), (128, 1024))
        o_own = lax.dynamic_slice(o_rows, (0, r * 512), (128, 512))
        o_oth = lax.dynamic_slice(o_rows, (0, (1 - r) * 512), (128, 512))
        o_rows = jnp.concatenate([o_own, o_oth], axis=1)
        w_sub = (o_rows.astype(F32) + 0.5 * x_sum).astype(BF)
        w_got = [w_sub] + [hop(w_sub, m) for m in (1, 2, 3)]
        w_hole = []
        for n in range(4):
            sel = jnp.where(c ^ n == 2, w_got[2], w_got[3])
            w_hole.append(jnp.where(c ^ n == 0, w_got[0], jnp.where(c ^ n == 1, w_got[1], sel)))
        w_hole = jnp.concatenate(w_hole, axis=0)
        rhs_lo = jnp.concatenate([half(t_a, r), half(t_b, r), s_a, s_b], axis=1)
        p_lo = mm(vv_t, rhs_lo, ((1,), (0,)))
        w_both = jnp.concatenate([w_hole[:, :512], swap(w_hole[:, 512:])], axis=0)
        r2v = mm(t_cat, w_both, ((1,), (0,))) + v_t.astype(F32)
        q_lo = swap(p_lo)
        t_hi, w_out, d_out, p_lo = fence((t_hi, w_out, d_out, p_lo))
        w_got = [hop(x, m) for m, x in enumerate(w_out, 1)]
        d_got = [hop(x, m) for m, x in enumerate(d_out, 1)]
        s_hi = swap(half(t_hi, 1 - r))
        mix_hi = mix(t_hi.reshape(144, 144, 256)).reshape(1152, 4608)
        rhs_hi = jnp.concatenate([half(t_hi, r), s_hi], axis=1)
        p_hi = mm(vv_t, rhs_hi, ((1,), (0,)))
        q_hi = swap(p_hi)
        w_oth = [swap(x) for x in w_got]
        idx = jnp.stack([2 * c, 2 * c + 1] + [2 * (c ^ m) + r for m in (1, 2, 3)] + [2 * (c ^ m) + 1 - r for m in (1, 2, 3)] + [c])
        w_img = place(idx, wt_all, [x[None] for x in w_got], [x[None] for x in w_oth]).reshape(1152, 4608)
        im_lo = mm(w_img, mix_lo, ((1,), (1,))).reshape(2, 2, 36, 8, 1152)
        im_hi = mm(w_img, mix_hi, ((1,), (1,))).reshape(2, 2, 36, 8, 1152)
        imgs = [im_lo, im_hi, swap(pick(im_lo, 1 - r))[None], swap(pick(im_hi, 1 - r))[None]]
        shape = (36, 144, 512)
        rv = r.reshape(1)
        r2v = r2v.reshape(shape)
        b_lo = regroup_base(0, rv, p_lo.reshape(shape), q_lo.reshape(shape), r2v, imgs)
        b_lo = [pick(b_lo, c ^ m) for m in range(4)]
        lo_got = [hop(b_lo[m], m) for m in (1, 2, 3)]
        b_hi = regroup_base(1, rv, p_hi.reshape(shape), q_hi.reshape(shape), r2v, imgs)
        b_hi = [pick(b_hi, c ^ m) for m in range(4)]
        hi_got = [hop(b_hi[m], m) for m in (1, 2, 3)]
        r3_lo = mm(mix_lo, w_blk, ((1,), (0,))).reshape(8, 144, 1152)
        r3_hi = mm(mix_hi, w_blk, ((1,), (0,))).reshape(8, 144, 1152)
        cv = c.reshape(1)
        out = finish(0, cv, b_lo[0], lo_got, d_all, d_got, r3_lo)
        out = finish(1, cv, b_hi[0], hi_got, d_all, d_got, r3_hi, out)
        return out.reshape(2304, 1152)

    return jax.shard_map(
        sweep,
        mesh=mesh,
        in_specs=(P("row", "col"), P("row", "col"), P("row", "col"), P("row", "col"), P(None, None), P(None, "col")),
        out_specs=P("row", "col"),
        check_vma=False,
    )
```

time: 1830 us -> 783 us (0.43)
  local copies, waits for them, and re-layouts: 625 us -> 52.8 us
  blocking collectives: 458 us -> 0 us
  Pallas kernels: 0 us -> 171 us
  other arithmetic: 166 us -> 9.13 us
  waiting for transfers between devices: 302 us -> 272 us
    all_to_all x3 -> x0, blocking collectives: 458 us -> none  [the longest x1 210 us: local_sweep(): t_pairs = lax.all_to_all(total_sum, 'col', 2, 1, tiled=True)]
    ppermute x0 -> x30, waiting for transfers between devices: none -> 217 us  [the longest x18 205 us: hop(): return lax.ppermute(x, 'col', [(i, i ^ m) for i in range(col_n)])]
    all_to_all x10 -> x0, local copies, waits for them, and re-layouts: 195 us -> none  [the longest x3 76.1 us: local_sweep(): swap_full = lax.all_to_all(swap_rows, 'col', 3, 1, tiled=True)]
    pallas_call x0 -> x10, Pallas kernels: none -> 171 us  [the longest x3 67.5 us: mix(): pl.pallas_call(functools.partial(mix_kernel, nb=nb, nj=nj, pitch=pitch),...]
    unnamed x7 -> x34, local copies, waits for them, and re-layouts: 161 us -> 4.03 us
    all_gather x2 -> x3, waiting for transfers between devices: 204 us -> 54 us  [the longest x1 31.9 us: sweep(): t_b = gather(t_own[:, 128:256])]
    reshape x5 -> x0, local copies, waits for them, and re-layouts: 137 us -> none  [the longest x1 67.4 us: local_sweep(): amp_four = t_rows.reshape(occ_r, n_occ, n_vir, n_vir)]
    all_to_all x1 -> x0, other arithmetic: 115 us -> none  [local_sweep(): swap_full = lax.all_to_all(swap_rows, 'col', 3, 1, tiled=True)]
  transfers between devices with their start and end apart: 7 -> 33, of which waited for: 4 -> 9; matrix products, arithmetic and copies ran while one was open for 46% -> 35% of each run, Pallas kernels for 0% -> 20%
where the time goes in v1:
time: 783 us; the launch traced here: 775 us
  waiting for transfers between devices  272 us (35%)
  matrix products  232 us (30%)
  Pallas kernels  171 us (22%)
  local copies, waits for them, and re-layouts  52.8 us (7%)
  starting transfers between devices  24.5 us (3%)
  between operations  13.7 us (2%)
  other arithmetic  9.13 us (1%)
    dot_general x8, matrix products, mm(): return lax.dot_general(a, b, (dims, ((), ())), preferred_element_type=F32)  232 us
    ppermute x18, waiting for transfers between devices, hop(): return lax.ppermute(x, 'col', [(i, i ^ m) for i in range(col_n)])  205 us
    pallas_call x3, Pallas kernels, mix(): pl.pallas_call(functools.partial(mix_kernel, nb=nb, nj=nj, pitch=pitch),...  67.5 us
    pallas_call x2, Pallas kernels, regroup_base(): pl.pallas_call(functools.partial(base_kernel, na=na, pitch=pitch), grid_s...  32.1 us
    all_gather x1, waiting for transfers between devices, sweep(): t_b = gather(t_own[:, 128:256])  31.9 us
    pallas_call x2, Pallas kernels, finish(): pl.pallas_call(fin_kernel, grid_spec=pltpu.PrefetchScalarGridSpec(num_sca...  24.6 us
    squeeze x7, local copies, waits for them, and re-layouts, pick(): return lax.dynamic_index_in_dim(x, i, 0, keepdims=False)  24.2 us
    all_gather x1, waiting for transfers between devices, sweep(): t_hi = gather(t_own[:, 256:])  22.1 us
  transfers between devices with their start and end apart: 33, of which 9 were waited for; matrix products, arithmetic and copies ran while one was open for 35% of the time, Pallas kernels for 20%

profile of v1, /device:TPU:0, one launch (start us, length us, event | category | flops | bytes accessed | tf_op | source)
XLA Modules:
  0.0 774.9 jit_solution(14754277502191666565)
XLA Ops:
  6.5 4.7 convert_bitcast_fusion
  20.6 17.2 %shard_map.65.d0 = f32[4,2,36,8,1152]{4,3,2,1,0:T(8,128)} custom-call(f32[36,144,512]{2,1,0:T(8,128)} %bitcast.123), custom_call_target="tpu_custom_call" | custom-call | flops 1020000000 | bytes 21233664 | tf_op jit(solution)/shard_map/pallas_call | solution.py:38
  37.9 19.1 %shard_map.64 = bf16[1152,4608]{1,0:T(8,128)(2,1)} custom-call(bf16[4608,1152]{1,0:T(8,128)(2,1)} %w_ref.1), custom_call_target="tpu_custom_call" | custom-call | flops 1140000000 | bytes 21233664 | tf_op jit(solution)/shard_map/pallas_call | solution.py:140
  57.0 6.8 dynamic-slice_bitcast_fusion.2
  67.9 8.7 %fusion.19 = f32[1024,512]{0,1:T(8,128)S(1)} fusion(bf16[512,5184]{0,1:T(8,128)(2,1)} %param.8, bf16[5184,512]{1,0:T(8,128)(2,1)} %collective-permute-done, bf16[5184,512]{1,0:T(8,128)(2,1)S(1)} %bitcast.119), kind=kOutput, calls=%fused_computation.19 | convolution fusion | flops 5457051648 | bytes 18022400 | tf_op jit(solution)/shard_map/dot_general | solution.py:234
  81.7 19.3 %shard_map.66.rest_0_ = bf16[8,144,4608]{2,1,0:T(8,128)(2,1)} custom-call(bf16[144,144,128]{2,1,0:T(8,128)(2,1)} %bitcast.122), custom_call_target="tpu_custom_call" | custom-call | flops 864000000 | bytes 10616832 | tf_op jit(solution)/shard_map/pallas_call | solution.py:119
  101.0 31.9 %all-gather.8.cloned.1.call-done = bf16[20736,128]{1,0:T(8,128)(2,1)} async-done(((bf16[5184,128]{1,0:T(8,128)(2,1)}), bf16[20736,128]{1,0:T(8,128)(2,1)}) %all-gather.8.cloned.1.call-update) | async-done | bytes 5308432 | tf_op jit(solution)/shard_map/all_gather | solution.py:245
  136.7 4.9 collective-permute-done.2
  143.2 69.9 %fusion.16 = f32[5184,512]{1,0:T(8,128)} fusion(bf16[10368,5184]{0,1:T(8,128)(2,1)} %param.9, bf16[10368,128]{1,0:T(8,128)(2,1)} %copy-done.12, bf16[10368,128]{1,0:T(8,128)(2,1)} %collective-permute-done.1, bf16[10368,128]{1,0:T(8,128)(2,1)} %get-tuple-element.73, bf16[10368,128]{1,0:T(8,128)(2,1)S(1)} %get-tuple-element.71), kind=kOutput, calls=%fused_computation.18 | convolution fusion | flops 55080124416 | bytes 128729088 | tf_op jit(solution)/shard_map/dot_general | solution.py:234
  213.1 22.1 %all-gather.4.cloned.1.call-done = bf16[20736,256]{1,0:T(8,128)(2,1)} async-done(((bf16[5184,256]{1,0:T(8,128)(2,1)}), bf16[20736,256]{1,0:T(8,128)(2,1)}) %all-gather.4.cloned.1.call-update) | async-done | bytes 10616848 | tf_op jit(solution)/shard_map/all_gather | solution.py:246
  235.2 9.9 %constant_dynamic-slice_fusion.1 = (bf16[10368,256]{1,0:T(8,128)(2,1)}, bf16[10368,256]{1,0:T(8,128)(2,1)}) fusion(bf16[20736,256]{1,0:T(8,128)(2,1)} %all-gather.4.cloned.1.call-done, s32[]{:T(128)S(6)} %select_n.147, s32[]{:T(128)S(6)} %select_n.148), kind=kLoop, calls=%fused_computation.51 | loop fusion | bytes 21233672 | tf_op jit(solution)/shard_map/dynamic_slice | solution.py:253
  250.1 66.5 %collective-permute-done.5 = f32[128,1024]{1,0:T(8,128)S(1)} collective-permute-done((f32[128,1024]{1,0:T(8,128)S(1)}, f32[128,1024]{1,0:T(8,128)S(1)}, u32[]{:S(2)}, u32[]{:S(2)}) %collective-permute-start.5) | collective-permute-done | bytes 524320 | tf_op jit(solution)/shard_map/ppermute | solution.py:225
  318.6 11.5 %collective-permute-done.6 = f32[128,1024]{1,0:T(8,128)} collective-permute-done((f32[128,1024]{1,0:T(8,128)S(1)}, f32[128,1024]{1,0:T(8,128)}, u32[]{:S(2)}, u32[]{:S(2)}) %collective-permute-start.6) | collective-permute-done | bytes 524320 | tf_op jit(solution)/shard_map/ppermute | solution.py:225
  333.4 19.3 %shard_map.68 = bf16[8,144,4608]{2,1,0:T(8,128)(2,1)} custom-call(bf16[144,144,128]{2,1,0:T(8,128)(2,1)} %bitcast.117, bf16[8,144,4608]{2,1,0:T(8,128)(2,1)} %shard_map.66.rest_0_), custom_call_target="tpu_custom_call", output_to_operand_aliasing={{}: (1, {})} | custom-call | flops 864000000 | bytes 10616832 | tf_op jit(solution)/shard_map/pallas_call | solution.py:119
  356.4 28.9 %shard_map.69 = bf16[8,144,4608]{2,1,0:T(8,128)(2,1)} custom-call(bf16[144,144,256]{2,1,0:T(8,128)(2,1)} %bitcast.114), custom_call_target="tpu_custom_call" | custom-call | flops 1728000000 | bytes 21233664 | tf_op jit(solution)/shard_map/pallas_call | solution.py:119
  387.3 10.0 %shard_map.67 = bf16[8,144,4608]{2,1,0:T(8,128)(2,1)} custom-call(s32[9]{0:T(128)} %stack.36.s_ref, bf16[8,144,4608]{2,1,0:T(8,128)(2,1)} %bitcast.111, bf16[8,144,4608]{2,1,0:T(8,128)(2,1)} %bitcast.112, bf16[1,144,4608]{2,1,0:T(8,128)(2,1)} %bitcast.131, bf16[1,144,4608]{2,1,0:T(8,128)(2,1)} %bitcast.132, bf16[1,144,4608]{2,1,0:T(8,128)(2,1)} %bitcast.36.refs_4_, ...), custom_call_target="tpu_custom_call" | custom-call | flops 480000000 | bytes 21233664 | tf_op jit(solution)/shard_map/pallas_call | solution.py:165
  397.3 66.9 %fusion.8 = f32[512,5184]{0,1:T(8,128)} fusion(bf16[10368,5184]{0,1:T(8,128)(2,1)} %param.9, bf16[10368,256]{1,0:T(8,128)(2,1)} %collective-permute-done.3, bf16[10368,256]{1,0:T(8,128)(2,1)} %get-tuple-element.55), kind=kOutput, calls=%fused_computation.9 | convolution fusion | flops 55058890752 | bytes 128729088 | tf_op jit(solution)/shard_map/dot_general | solution.py:234
  464.7 17.8 %fusion.31.ah = f32[2,2,36,8,1152]{4,3,2,1,0:T(8,128)S(1)} fusion(bf16[2,2,36,8,4608]{4,3,2,1,0:T(8,128)(2,1)} %bitcast.128, bf16[1152,4608,1,1,1]{1,0,4,3,2:T(8,128)(2,1)} %bitcast.124), kind=kOutput, calls=%fused_computation.64 | convolution fusion | flops 12230590464 | bytes 26542080 | tf_op jit(solution)/shard_map/dot_general | solution.py:234
  484.3 19.0 %fusion.30.al = f32[2,2,36,8,1152]{4,3,2,1,0:T(8,128)S(1)} fusion(bf16[2,2,36,8,4608]{4,3,2,1,0:T(8,128)(2,1)} %bitcast.129, bf16[1152,4608,1,1,1]{1,0,4,3,2:T(8,128)(2,1)} %bitcast.113), kind=kOutput, calls=%fused_computation.63 | convolution fusion | flops 12230590464 | bytes 26542080 | tf_op jit(solution)/shard_map/dot_general | solution.py:234
  506.4 6.8 collective-permute-done.11
  513.2 10.8 %bitcast_add_fusion = f32[5184,512]{1,0:T(8,128)} fusion(bf16[512,5184]{0,1:T(8,128)(2,1)} %param.8, bf16[5184,512]{1,0:T(8,128)(2,1)} %collective-permute-done, bf16[5184,512]{1,0:T(8,128)(2,1)S(1)} %bitcast.121, bf16[512,512]{1,0:T(8,128)(2,1)S(1)} %collective-permute-done.11, bf16[512,512]{1,0:T(8,128)(2,1)S(1)} %get-tuple-element.83), kind=kOutput, calls=%fused_computation.17 | convolution fusion | flops 5464457216 | bytes 27590656 | tf_op jit(solution)/shard_map/dot_general | solution.py:234
  527.5 16.0 %shard_map.71 = f32[4,36,8,1152]{3,2,1,0:T(8,128)} custom-call(s32[1]{0:T(128)} %bitcast.1.s_ref, f32[36,144,512]{2,1,0:T(8,128)} %bitcast.125, f32[36,144,512]{2,1,0:T(8,128)} %bitcast.59.q_ref, f32[36,144,512]{2,1,0:T(8,128)} %bitcast.115, f32[2,2,36,8,1152]{4,3,2,1,0:T(8,128)} %copy-done.1, f32[2,2,36,8,1152]{4,3,2,1,0:T(8,128)} %copy-done, ...), custom_call_target="tpu_custom_call" | custom-call | flops 960000000 | bytes 26542080 | tf_op jit(solution)/shard_map/pallas_call | solution.py:75
  543.5 4.9 dynamic-slice_bitcast_fusion.5
  549.8 19.7 %fusion.12.r_ref = f32[8,144,1152]{2,1,0:T(8,128)} fusion(bf16[8,144,4608]{2,1,0:T(8,128)(2,1)} %shard_map.68, bf16[4608,1152]{1,0:T(8,128)(2,1)} %w_ref.1), kind=kOutput, calls=%fused_computation.13 | convolution fusion | flops 12230590464 | bytes 26542080 | tf_op jit(solution)/shard_map/dot_general | solution.py:234
  571.0 16.1 %shard_map.70 = f32[4,36,8,1152]{3,2,1,0:T(8,128)} custom-call(s32[1]{0:T(128)} %bitcast.1.s_ref, f32[36,144,512]{2,1,0:T(8,128)} %bitcast.127, f32[36,144,512]{2,1,0:T(8,128)} %bitcast.23.q_ref, f32[36,144,512]{2,1,0:T(8,128)} %bitcast.116, f32[2,2,36,8,1152]{4,3,2,1,0:T(8,128)} %copy-done.1, f32[2,2,36,8,1152]{4,3,2,1,0:T(8,128)} %copy-done, ...), custom_call_target="tpu_custom_call" | custom-call | flops 960000000 | bytes 26542080 | tf_op jit(solution)/shard_map/pallas_call | solution.py:75
  587.2 5.3 dynamic-slice_bitcast_fusion.9
  593.0 78.5 %collective-permute-done.24.d2 = f32[2,36,8,1152]{3,2,1,0:T(8,128)} collective-permute-done((f32[2,36,8,1152]{3,2,1,0:T(8,128)}, f32[2,36,8,1152]{3,2,1,0:T(8,128)}, u32[]{:S(2)}, u32[]{:S(2)}) %collective-permute-start.24) | collective-permute-done | bytes 2654240 | tf_op jit(solution)/shard_map/ppermute | solution.py:225
  675.0 19.7 %fusion.14.r_ref = f32[8,144,1152]{2,1,0:T(8,128)} fusion(bf16[8,144,4608]{2,1,0:T(8,128)(2,1)} %shard_map.69, bf16[4608,1152]{1,0:T(8,128)(2,1)} %w_ref.1), kind=kOutput, calls=%fused_computation.15 | convolution fusion | flops 12230590464 | bytes 26542080 | tf_op jit(solution)/shard_map/dot_general | solution.py:234
  694.8 33.7 %collective-permute-done.28.b2 = f32[36,8,1152]{2,1,0:T(8,128)} collective-permute-done((f32[36,8,1152]{2,1,0:T(8,128)}, f32[36,8,1152]{2,1,0:T(8,128)}, u32[]{:S(2)}, u32[]{:S(2)}) %collective-permute-start.28) | collective-permute-done | bytes 1327136 | tf_op jit(solution)/shard_map/ppermute | solution.py:225
  728.4 12.3 %shard_map.72.rest_0_ = f32[16,144,1152]{2,1,0:T(8,128)} custom-call(s32[1]{0:T(128)} %bitcast.c_ref, f32[36,8,1152]{2,1,0:T(8,128)} %get-tuple-element.66.b0, f32[36,8,1152]{2,1,0:T(8,128)} %collective-permute-done.27.b1, f32[36,8,1152]{2,1,0:T(8,128)} %collective-permute-done.28.b2, f32[36,8,1152]{2,1,0:T(8,128)} %collective-permute-done.29.b3, ...), custom_call_target="tpu_custom_call" | custom-call | flops 600000000 | bytes 21233664 | tf_op jit(solution)/shard_map/pallas_call | solution.py:205
  740.8 15.0 %collective-permute-done.21.b2 = f32[36,8,1152]{2,1,0:T(8,128)} collective-permute-done((f32[36,8,1152]{2,1,0:T(8,128)}, f32[36,8,1152]{2,1,0:T(8,128)}, u32[]{:S(2)}, u32[]{:S(2)}) %collective-permute-start.21) | collective-permute-done | bytes 1327136 | tf_op jit(solution)/shard_map/ppermute | solution.py:225
  755.8 12.3 %shard_map.73 = f32[16,144,1152]{2,1,0:T(8,128)} custom-call(s32[1]{0:T(128)} %bitcast.c_ref, f32[36,8,1152]{2,1,0:T(8,128)} %get-tuple-element.70.b0, f32[36,8,1152]{2,1,0:T(8,128)} %collective-permute-done.20.b1, f32[36,8,1152]{2,1,0:T(8,128)} %collective-permute-done.21.b2, ...), custom_call_target="tpu_custom_call", output_to_operand_aliasing={{}: (10, {})} | custom-call | flops 600000000 | bytes 21233664 | tf_op jit(solution)/shard_map/pallas_call | solution.py:205
  (110 shorter events, 55.6 us)
Async XLA Ops:
  6.5 71.3 %all-gather.6.cloned.1.call-start = ((), (), s32[]{:S(2)}) async-start(), calls=%async_computation.1 | async-start | bytes 6635520 | tf_op jit(solution)/shard_map/all_gather | solution.py:244
  15.4 117.5 %all-gather.8.cloned.1.call-start = ((), (), s32[]{:S(2)}) async-start(), calls=%async_computation.2 | async-start | bytes 6635520 | tf_op jit(solution)/shard_map/all_gather | solution.py:245
  16.2 219.0 %all-gather.4.cloned.1.call-start = ((), (), s32[]{:S(2)}) async-start(), calls=%async_computation | async-start | bytes 13271040 | tf_op jit(solution)/shard_map/all_gather | solution.py:246
  16.2 51.6 %collective-permute-start = (bf16[5184,512]{1,0:T(8,128)(2,1)}, bf16[5184,512]{1,0:T(8,128)(2,1)}, u32[]{:S(2)}, u32[]{:S(2)}) collective-permute-start(bf16[5184,512]{1,0:T(8,128)(2,1)} %copy-done.2), channel_id=1, source_target_pairs={{0,1},{1,0},{2,3},{3,2},{4,5},{5,4},{6,7},{7,6}} | collective-permute-start | bytes 15925256 | tf_op jit(solution)/shard_map/ppermute | solution.py:228
  81.7 55.0 %collective-permute-start.1 = (bf16[10368,128]{1,0:T(8,128)(2,1)}, bf16[10368,128]{1,0:T(8,128)(2,1)}, u32[]{:S(2)}, u32[]{:S(2)}) collective-permute-start(bf16[10368,128]{1,0:T(8,128)(2,1)} %get-tuple-element.72), channel_id=1, source_target_pairs={{0,1},{1,0},{2,3},{3,2},{4,5},{5,4},{6,7},{7,6}} | collective-permute-start | bytes 7962632 | tf_op jit(solution)/shard_map/ppermute | solution.py:228
  245.1 152.1 %collective-permute-start.3 = (bf16[10368,256]{1,0:T(8,128)(2,1)}, bf16[10368,256]{1,0:T(8,128)(2,1)}, u32[]{:S(2)}, u32[]{:S(2)}) collective-permute-start(bf16[10368,256]{1,0:T(8,128)(2,1)} %get-tuple-element.56), channel_id=1, source_target_pairs={{0,1},{1,0},{2,3},{3,2},{4,5},{5,4},{6,7},{7,6}} | collective-permute-start | bytes 15925256 | tf_op jit(solution)/shard_map/ppermute | solution.py:228
  245.1 72.9 %collective-permute-start.12 = (bf16[144,4608]{1,0:T(8,128)(2,1)}, bf16[144,4608]{1,0:T(8,128)(2,1)S(1)}, u32[]{:S(2)}, u32[]{:S(2)}) collective-permute-start(bf16[144,4608]{1,0:T(8,128)(2,1)} %get-tuple-element.47), channel_id=1, source_target_pairs={{0,2},{2,0},{4,6},{6,4},{1,3},{3,1},{5,7},{7,5}} | collective-permute-start | bytes 3981320 | tf_op jit(solution)/shard_map/ppermute | solution.py:225
  246.6 71.5 %collective-permute-start.13 = (bf16[144,4608]{1,0:T(8,128)(2,1)S(1)}, bf16[144,4608]{1,0:T(8,128)(2,1)S(1)}, u32[]{:S(2)}, u32[]{:S(2)}) collective-permute-start(bf16[144,4608]{1,0:T(8,128)(2,1)S(1)} %copy-done.7), channel_id=1, source_target_pairs={{0,4},{2,6},{4,0},{6,2},{1,5},{3,7},{5,1},{7,3}} | collective-permute-start | bytes 3981320 | tf_op jit(solution)/shard_map/ppermute | solution.py:225
  247.2 71.4 %collective-permute-start.14 = (bf16[144,4608]{1,0:T(8,128)(2,1)S(1)}, bf16[144,4608]{1,0:T(8,128)(2,1)}, u32[]{:S(2)}, u32[]{:S(2)}) collective-permute-start(bf16[144,4608]{1,0:T(8,128)(2,1)S(1)} %copy-done.6), channel_id=1, source_target_pairs={{0,6},{2,4},{4,2},{6,0},{1,7},{3,5},{5,3},{7,1}} | collective-permute-start | bytes 3981320 | tf_op jit(solution)/shard_map/ppermute | solution.py:225
  248.6 67.9 %collective-permute-start.5 = (f32[128,1024]{1,0:T(8,128)S(1)}, f32[128,1024]{1,0:T(8,128)S(1)}, u32[]{:S(2)}, u32[]{:S(2)}) collective-permute-start(f32[128,1024]{1,0:T(8,128)S(1)} %copy-done.11), channel_id=1, source_target_pairs={{0,2},{2,0},{4,6},{6,4},{1,3},{3,1},{5,7},{7,5}} | collective-permute-start | bytes 1572872 | tf_op jit(solution)/shard_map/ppermute | solution.py:225
  316.6 13.6 %collective-permute-start.6 = (f32[128,1024]{1,0:T(8,128)S(1)}, f32[128,1024]{1,0:T(8,128)}, u32[]{:S(2)}, u32[]{:S(2)}) collective-permute-start(f32[128,1024]{1,0:T(8,128)S(1)} %copy-done.10), channel_id=1, source_target_pairs={{0,4},{2,6},{4,0},{6,2},{1,5},{3,7},{5,1},{7,3}} | collective-permute-start | bytes 1572872 | tf_op jit(solution)/shard_map/ppermute | solution.py:225
  318.1 67.2 %collective-permute-start.15 = (bf16[144,4608]{1,0:T(8,128)(2,1)S(1)}, bf16[144,4608]{1,0:T(8,128)(2,1)}, u32[]{:S(2)}, u32[]{:S(2)}) collective-permute-start(bf16[144,4608]{1,0:T(8,128)(2,1)S(1)} %collective-permute-done.12), channel_id=1, source_target_pairs={{0,1},{1,0},{2,3},{3,2},{4,5},{5,4},{6,7},{7,6}} | collective-permute-start | bytes 3981320 | tf_op jit(solution)/shard_map/ppermute | solution.py:228
  318.1 68.7 %collective-permute-start.16 = (bf16[144,4608]{1,0:T(8,128)(2,1)S(1)}, bf16[144,4608]{1,0:T(8,128)(2,1)}, u32[]{:S(2)}, u32[]{:S(2)}) collective-permute-start(bf16[144,4608]{1,0:T(8,128)(2,1)S(1)} %collective-permute-done.13), channel_id=1, source_target_pairs={{0,1},{1,0},{2,3},{3,2},{4,5},{5,4},{6,7},{7,6}} | collective-permute-start | bytes 3981320 | tf_op jit(solution)/shard_map/ppermute | solution.py:228
  318.6 68.7 %collective-permute-start.17 = (bf16[144,4608]{1,0:T(8,128)(2,1)}, bf16[144,4608]{1,0:T(8,128)(2,1)}, u32[]{:S(2)}, u32[]{:S(2)}) collective-permute-start(bf16[144,4608]{1,0:T(8,128)(2,1)} %collective-permute-done.14), channel_id=1, source_target_pairs={{0,1},{1,0},{2,3},{3,2},{4,5},{5,4},{6,7},{7,6}} | collective-permute-start | bytes 3981320 | tf_op jit(solution)/shard_map/ppermute | solution.py:228
  330.2 22.5 %collective-permute-start.7 = (f32[128,1024]{1,0:T(8,128)}, f32[128,1024]{1,0:T(8,128)}, u32[]{:S(2)}, u32[]{:S(2)}) collective-permute-start(f32[128,1024]{1,0:T(8,128)} %get-tuple-element.46), channel_id=1, source_target_pairs={{0,6},{2,4},{4,2},{6,0},{1,7},{3,5},{5,3},{7,1}} | collective-permute-start | bytes 1572872 | tf_op jit(solution)/shard_map/ppermute | solution.py:225
  354.9 148.6 %collective-permute-start.10 = (bf16[128,1024]{1,0:T(8,128)(2,1)}, bf16[128,1024]{1,0:T(8,128)(2,1)}, u32[]{:S(2)}, u32[]{:S(2)}) collective-permute-start(bf16[128,1024]{1,0:T(8,128)(2,1)} %add_convert_fusion), channel_id=1, source_target_pairs={{0,6},{2,4},{4,2},{6,0},{1,7},{3,5},{5,3},{7,1}} | collective-permute-start | bytes 786440 | tf_op jit(solution)/shard_map/ppermute | solution.py:225
  385.3 118.3 %collective-permute-start.9 = (bf16[128,1024]{1,0:T(8,128)(2,1)}, bf16[128,1024]{1,0:T(8,128)(2,1)}, u32[]{:S(2)}, u32[]{:S(2)}) collective-permute-start(bf16[128,1024]{1,0:T(8,128)(2,1)} %add_convert_fusion), channel_id=1, source_target_pairs={{0,4},{2,6},{4,0},{6,2},{1,5},{3,7},{5,1},{7,3}} | collective-permute-start | bytes 786440 | tf_op jit(solution)/shard_map/ppermute | solution.py:225
  386.7 117.3 %collective-permute-start.8 = (bf16[128,1024]{1,0:T(8,128)(2,1)}, bf16[128,1024]{1,0:T(8,128)(2,1)}, u32[]{:S(2)}, u32[]{:S(2)}) collective-permute-start(bf16[128,1024]{1,0:T(8,128)(2,1)} %add_convert_fusion), channel_id=1, source_target_pairs={{0,2},{2,0},{4,6},{6,4},{1,3},{3,1},{5,7},{7,5}} | collective-permute-start | bytes 786440 | tf_op jit(solution)/shard_map/ppermute | solution.py:225
  387.3 140.2 %collective-permute-start.26 = (f32[5184,512]{1,0:T(8,128)}, f32[5184,512]{1,0:T(8,128)}, u32[]{:S(2)}, u32[]{:S(2)}) collective-permute-start(f32[5184,512]{1,0:T(8,128)} %fusion.16), channel_id=1, source_target_pairs={{0,1},{1,0},{2,3},{3,2},{4,5},{5,4},{6,7},{7,6}} | collective-permute-start | bytes 31850504 | tf_op jit(solution)/shard_map/ppermute | solution.py:228
  464.2 105.4 %collective-permute-start.4 = (f32[5184,512]{1,0:T(8,128)}, f32[5184,512]{1,0:T(8,128)}, u32[]{:S(2)}, u32[]{:S(2)}) collective-permute-start(f32[5184,512]{1,0:T(8,128)} %bitcast.126), channel_id=1, source_target_pairs={{0,1},{1,0},{2,3},{3,2},{4,5},{5,4},{6,7},{7,6}} | collective-permute-start | bytes 31850504 | tf_op jit(solution)/shard_map/ppermute | solution.py:228
  503.5 22.0 %collective-permute-start.19 = (f32[2,36,8,1152]{3,2,1,0:T(8,128)}, f32[2,36,8,1152]{3,2,1,0:T(8,128)}, u32[]{:S(2)}, u32[]{:S(2)}) collective-permute-start(f32[2,36,8,1152]{3,2,1,0:T(8,128)} %dynamic-slice_bitcast_fusion), channel_id=1, source_target_pairs={{0,1},{1,0},{2,3},{3,2},{4,5},{5,4},{6,7},{7,6}} | collective-permute-start | bytes 7962632 | tf_op jit(solution)/shard_map/ppermute | solution.py:228
  503.6 22.5 %collective-permute-start.18 = (f32[2,36,8,1152]{3,2,1,0:T(8,128)S(1)}, f32[2,36,8,1152]{3,2,1,0:T(8,128)}, u32[]{:S(2)}, u32[]{:S(2)}) collective-permute-start(f32[2,36,8,1152]{3,2,1,0:T(8,128)S(1)} %dynamic-slice_bitcast_fusion.1), channel_id=1, source_target_pairs={{0,1},{1,0},{2,3},{3,2},{4,5},{5,4},{6,7},{7,6}} | collective-permute-start | bytes 7962632 | tf_op jit(solution)/shard_map/ppermute | solution.py:228
  506.3 6.9 collective-permute-start.11
  524.0 68.4 %collective-permute-start.23 = (f32[2,36,8,1152]{3,2,1,0:T(8,128)}, f32[2,36,8,1152]{3,2,1,0:T(8,128)S(1)}, u32[]{:S(2)}, u32[]{:S(2)}) collective-permute-start(f32[2,36,8,1152]{3,2,1,0:T(8,128)} %get-tuple-element.51), channel_id=1, source_target_pairs={{0,2},{2,0},{4,6},{6,4},{1,3},{3,1},{5,7},{7,5}} | collective-permute-start | bytes 7962632 | tf_op jit(solution)/shard_map/ppermute | solution.py:225
  525.5 146.1 %collective-permute-start.24 = (f32[2,36,8,1152]{3,2,1,0:T(8,128)}, f32[2,36,8,1152]{3,2,1,0:T(8,128)}, u32[]{:S(2)}, u32[]{:S(2)}) collective-permute-start(f32[2,36,8,1152]{3,2,1,0:T(8,128)} %get-tuple-element.52), channel_id=1, source_target_pairs={{0,4},{2,6},{4,0},{6,2},{1,5},{3,7},{5,1},{7,3}} | collective-permute-start | bytes 7962632 | tf_op jit(solution)/shard_map/ppermute | solution.py:225
  526.0 147.0 %collective-permute-start.25 = (f32[2,36,8,1152]{3,2,1,0:T(8,128)}, f32[2,36,8,1152]{3,2,1,0:T(8,128)}, u32[]{:S(2)}, u32[]{:S(2)}) collective-permute-start(f32[2,36,8,1152]{3,2,1,0:T(8,128)} %get-tuple-element.53), channel_id=1, source_target_pairs={{0,6},{2,4},{4,2},{6,0},{1,7},{3,5},{5,3},{7,1}} | collective-permute-start | bytes 7962632 | tf_op jit(solution)/shard_map/ppermute | solution.py:225
  548.4 125.2 %collective-permute-start.29 = (f32[36,8,1152]{2,1,0:T(8,128)}, f32[36,8,1152]{2,1,0:T(8,128)}, u32[]{:S(2)}, u32[]{:S(2)}) collective-permute-start(f32[36,8,1152]{2,1,0:T(8,128)} %get-tuple-element.63), channel_id=1, source_target_pairs={{0,6},{2,4},{4,2},{6,0},{1,7},{3,5},{5,3},{7,1}} | collective-permute-start | bytes 3981320 | tf_op jit(solution)/shard_map/ppermute | solution.py:225
  569.5 158.9 %collective-permute-start.28 = (f32[36,8,1152]{2,1,0:T(8,128)}, f32[36,8,1152]{2,1,0:T(8,128)}, u32[]{:S(2)}, u32[]{:S(2)}) collective-permute-start(f32[36,8,1152]{2,1,0:T(8,128)} %get-tuple-element.64), channel_id=1, source_target_pairs={{0,4},{2,6},{4,0},{6,2},{1,5},{3,7},{5,1},{7,3}} | collective-permute-start | bytes 3981320 | tf_op jit(solution)/shard_map/ppermute | solution.py:225
  592.4 136.0 %collective-permute-start.27 = (f32[36,8,1152]{2,1,0:T(8,128)S(1)}, f32[36,8,1152]{2,1,0:T(8,128)}, u32[]{:S(2)}, u32[]{:S(2)}) collective-permute-start(f32[36,8,1152]{2,1,0:T(8,128)S(1)} %copy-done.8), channel_id=1, source_target_pairs={{0,2},{2,0},{4,6},{6,4},{1,3},{3,1},{5,7},{7,5}} | collective-permute-start | bytes 3981320 | tf_op jit(solution)/shard_map/ppermute | solution.py:225
  671.5 69.2 %collective-permute-start.22 = (f32[36,8,1152]{2,1,0:T(8,128)}, f32[36,8,1152]{2,1,0:T(8,128)}, u32[]{:S(2)}, u32[]{:S(2)}) collective-permute-start(f32[36,8,1152]{2,1,0:T(8,128)} %get-tuple-element.67), channel_id=1, source_target_pairs={{0,6},{2,4},{4,2},{6,0},{1,7},{3,5},{5,3},{7,1}} | collective-permute-start | bytes 3981320 | tf_op jit(solution)/shard_map/ppermute | solution.py:225
  673.0 82.7 %collective-permute-start.21 = (f32[36,8,1152]{2,1,0:T(8,128)}, f32[36,8,1152]{2,1,0:T(8,128)}, u32[]{:S(2)}, u32[]{:S(2)}) collective-permute-start(f32[36,8,1152]{2,1,0:T(8,128)} %get-tuple-element.68), channel_id=1, source_target_pairs={{0,4},{2,6},{4,0},{6,2},{1,5},{3,7},{5,1},{7,3}} | collective-permute-start | bytes 3981320 | tf_op jit(solution)/shard_map/ppermute | solution.py:225
  673.6 82.2 %collective-permute-start.20 = (f32[36,8,1152]{2,1,0:T(8,128)}, f32[36,8,1152]{2,1,0:T(8,128)}, u32[]{:S(2)}, u32[]{:S(2)}) collective-permute-start(f32[36,8,1152]{2,1,0:T(8,128)} %get-tuple-element.69), channel_id=1, source_target_pairs={{0,2},{2,0},{4,6},{6,4},{1,3},{3,1},{5,7},{7,5}} | collective-permute-start | bytes 3981320 | tf_op jit(solution)/shard_map/ppermute | solution.py:225
  (18 other events, 428.3 us)
Sparse Core Ops, SparseCore 0:
  15.6 59.0 all-gather.5
  76.4 56.4 all-gather.7
  134.7 100.4 all-gather.3
